TPU v7x, 32 devices: a whole 2x2x4 slice. The times are simulated.
32 devices in a mesh: gx: 4 (over z), gy: 8 (over y, x, core).
Axes of the slice: x: 2, y: 2, z: 4, core: 2. Of those that a mesh axis runs over, the one named last changes fastest.
Arguments:
- rhs: float32 [4, 8, 1, 3, 200, 128], P('gx', 'gy'), may hold values from -25 to 25
- stiff_inverse: bfloat16 [4, 8, 1, 1200, 1200], P('gx', 'gy'), may hold values from -2 to 6, as said below
- schur: bfloat16 [4, 8, 1, 1200, 1200], P('gx', 'gy'), may hold values from -2 to 6, as said below
- phi: bfloat16 [4, 8, 1, 24, 1200], P('gx', 'gy'), may hold values from -0.1875 to 0.1875
- coarse_inverse: float32 [192, 192], P(('gx', 'gy')), may hold values from -2 to 6, as said below
- incidence: int32 [4, 8, 1, 8], P('gx', 'gy'), may hold values from 0 to 63, as said below
- pairing: int32 [4, 8, 1, 3, 200], P('gx', 'gy'), may hold values from 0 to 199, as said below
Outputs:
- multipliers: float32 [4, 8, 1, 3, 200, 128], P('gx', 'gy')
- reduction: float32 [128], replicated
Inputs may be any that keep to these rules, and one draw needn't show every extreme that they name: `stiff_inverse`: each block is symmetric positive definite. `schur`: each block is symmetric positive definite. `coarse_inverse`: symmetric positive definite. `incidence`: the corners of the subdomain grid, periodic in the first two dimensions, under an arbitrary numbering of the 64 nodes: corner c of subdomain (x, y, z) is the grid point (x + c % 2, y + (c // 2) % 2, z + c // 4), and subdomains that share a grid point name the same node. `pairing`: each row over the last dimension is a permutation of 0 to 199.
All inputs are finite; a program needn't handle non-finite values.
Results may differ from a plain program's by a relative error of at most 0.0027.
Values sent between devices are 32-bit elements; how exact they have to be, the bound alone decides.
A program may use at most 64 MiB of HBM per device.

v0:
```python
import jax
import jax.numpy as jnp
from jax import lax
from jax.sharding import PartitionSpec as P

ITERS = 2
largest_index = lax.Precision.HIGHEST


def passed_along(array, axis, by):
    peers = lax.axis_size(axis)
    return lax.ppermute(array, axis, [(i, (i + by) % peers) for i in range(peers)])


def local(rhs, stiff_inverse, schur, phi, coarse_inverse, incidence, pairing):
    blocks = rhs.shape[2]
    face_dofs = rhs.shape[4]
    load_cases = rhs.shape[5]
    interface = 6 * face_dofs
    stiffness = stiff_inverse[0, 0]
    schur_block_stack = schur[0, 0]
    coupling_matrix = phi[0, 0].astype(jnp.float32)
    local_ids = incidence[0, 0]
    level = jnp.arange(blocks)[:, None]
    axis_id = jnp.arange(3)[None, :]
    active = jnp.where((level == blocks - 1) & (axis_id == 2), 0.0, 1.0).astype(jnp.float32)[
        :, :, None, None
    ]
    perm_table = (pairing[0, 0][..., None] == jnp.arange(face_dofs)[None, None, None, :]).astype(
        jnp.float32
    )
    owner_weights = None
    own_ids = jnp.concatenate([local_ids[:, 0], local_ids[-1:, 4]])
    own_dofs = (3 * own_ids[:, None] + jnp.arange(3, dtype=jnp.int32)[None, :]).reshape(-1)
    picked = jnp.take(
        lax.all_gather(coarse_inverse, ("gx", "gy"), axis=0, tiled=True), own_dofs, axis=1
    )
    every_owner = lax.all_gather(own_ids, ("gx", "gy"), axis=0, tiled=True)
    gathered_dofs = (3 * every_owner[:, None] + jnp.arange(3, dtype=jnp.int32)[None, :]).reshape(-1)
    owner_weights = jnp.take(picked, gathered_dofs, axis=0)

    def transpose_jump(values):
        masked = values * active
        moved = jnp.einsum("sakj,sakr->sajr", perm_table, masked, precision=largest_index)
        lower_x = passed_along(moved[:, 0], "gx", 1)
        lower_y = passed_along(moved[:, 1], "gy", 1)
        lower_z = jnp.concatenate([jnp.zeros_like(moved[:1, 2]), moved[:-1, 2]], axis=0)
        return jnp.stack(
            [-lower_x, masked[:, 0], -lower_y, masked[:, 1], -lower_z, masked[:, 2]], axis=1
        )

    def jump_field(field):
        upper_x = passed_along(field[:, 0], "gx", -1)
        upper_y = passed_along(field[:, 2], "gy", -1)
        upper_z = jnp.concatenate([field[1:, 4], jnp.zeros_like(field[:1, 4])], axis=0)
        neighbour = jnp.stack([upper_x, upper_y, upper_z], axis=1)
        paired = jnp.einsum("sakj,sajr->sakr", perm_table, neighbour, precision=largest_index)
        higher = jnp.stack([field[:, 1], field[:, 3], field[:, 5]], axis=1)
        return (higher - paired) * active

    def apply_local(matrices, field):
        low_field = field.reshape(blocks, interface, load_cases).astype(jnp.bfloat16)
        result = jnp.einsum("snm,smr->snr", matrices, low_field, preferred_element_type=jnp.float32)
        return result.reshape(blocks, 6, face_dofs, load_cases)

    def precondition(values):
        field = 0.5 * transpose_jump(values)
        return 0.5 * jump_field(apply_local(schur_block_stack, field))

    def inner_product(left, right):
        return jnp.sum(left * right, axis=(0, 1, 2))

    def energy_total(partial_value):
        return lax.psum(partial_value, ("gx", "gy"))

    residual = rhs[0, 0] * active
    multipliers = jnp.zeros_like(residual)
    preconditioned = precondition(residual)
    partial_energy = inner_product(residual, preconditioned)
    energy = energy_total(partial_energy)
    direction_field = None
    search_corner_values = None
    start_energy = energy
    direction = preconditioned
    for iteration in range(ITERS):
        direction_field = transpose_jump(direction)
        split = jnp.einsum(
            "vzh,vhq->vzq",
            coupling_matrix,
            direction_field.reshape(blocks, interface, load_cases),
            precision=largest_index,
        ).reshape(blocks, 2, 2, 2, 3, load_cases)
        empty = jnp.zeros((1, 2, 2, 3, load_cases), jnp.float32)
        by_node = jnp.concatenate([split[:, 0], empty], axis=0) + jnp.concatenate(
            [empty, split[:, 1]], axis=0
        )
        from_x = passed_along(by_node[:, :, 1], "gx", 1)
        along_x = by_node[:, :, 0] + from_x
        from_y = passed_along(along_x[:, 1], "gy", 1)
        owned = (along_x[:, 0] + from_y).reshape(-1, load_cases)
        gathered = lax.all_gather(owned, ("gx", "gy"), axis=0, tiled=True)
        solved = jnp.dot(owner_weights.T, gathered, precision=largest_index).reshape(
            blocks + 1, 3, load_cases
        )
        from_upper_x = passed_along(solved, "gx", -1)
        pair = jnp.stack([solved, from_upper_x], axis=0)
        from_upper_y = passed_along(pair, "gy", -1)
        quad = jnp.stack([pair, from_upper_y], axis=0)
        neighbour_values = jnp.stack([quad[:, :, :blocks], quad[:, :, 1:]], axis=0)
        neighbour_values = jnp.transpose(neighbour_values, (3, 0, 1, 2, 4, 5)).reshape(
            blocks, -1, load_cases
        )
        search_corner_values = neighbour_values
        spread_operator = jnp.einsum(
            "xgy,xgh->xyh", coupling_matrix, search_corner_values, precision=largest_index
        )
        displacement = apply_local(stiffness, direction_field) + spread_operator.reshape(
            blocks, 6, face_dofs, load_cases
        )
        product_field = jump_field(displacement)
        curvature = lax.psum(inner_product(direction, product_field), ("gx", "gy"))
        alpha = energy / curvature
        multipliers = multipliers + alpha * direction
        residual = residual - alpha * product_field
        preconditioned = precondition(residual)
        partial_energy = inner_product(residual, preconditioned)
        if iteration + 1 < ITERS:
            energy_next = energy_total(partial_energy)
            ratio = energy_next / energy
            direction = preconditioned + ratio * direction
        else:
            energy_next = energy_total(partial_energy)
        energy = energy_next
    return (multipliers[None, None], energy / start_energy)


def solution(mesh):
    return jax.shard_map(
        local,
        mesh=mesh,
        in_specs=(
            P("gx", "gy", None, None, None, None),
            P("gx", "gy", None, None, None),
            P("gx", "gy", None, None, None),
            P("gx", "gy", None, None, None),
            P(("gx", "gy"), None),
            P("gx", "gy", None, None),
            P("gx", "gy", None, None, None),
        ),
        out_specs=(P("gx", "gy", None, None, None, None), P()),
        check_vma=False,
    )
```

profile of v0, /device:TPU:0, one launch (start us, length us, event | category | flops | bytes accessed | tf_op | source)
XLA Modules:
  0.0 463.3 jit_solution(669811901619081959)
XLA Ops:
  4.6 2.6 collective-permute-start
  13.3 40.4 %all-reduce.4 = s32[64]{0:T(128)S(1)} all-reduce(s32[64]{0:T(128)S(1)} %fusion.96), channel_id=1, replica_groups=mesh['gx'=4,'gy'=8] {'gx','gy'}, use_global_device_ids=true, to_apply=%add.4 | all-reduce | flops 64 | bytes 512
  53.9 41.3 %all-gather = f32[32,6,192]{2,1,0:T(8,128)S(1)} all-gather(f32[1,6,192]{2,1,0:T(8,128)} %bitcast.317), channel_id=1, replica_groups=mesh['gx'=4,'gy'=8] {'gx','gy'}, dimensions={0}, use_global_device_ids=true | all-gather | bytes 152064 | tf_op jit(solution)/shard_map/all_gather | solution.py:36
  103.6 2.8 fusion
  106.6 5.0 %collective-permute-done.2 = f32[1,200,128]{2,1,0:T(8,128)S(1)} collective-permute-done((f32[1,200,128]{2,1,0:T(8,128)S(1)}, f32[1,200,128]{2,1,0:T(8,128)S(1)}, u32[]{:S(2)}, u32[]{:S(2)}) %collective-permute-start.2) | collective-permute-done | bytes 102432 | tf_op jit(solution)/shard_map/ppermute | solution.py:12
  114.1 5.6 %collective-permute-done.4 = f32[1,200,128]{2,1,0:T(8,128)S(1)} collective-permute-done((f32[1,200,128]{2,1,0:T(8,128)S(1)}, f32[1,200,128]{2,1,0:T(8,128)S(1)}, u32[]{:S(2)}, u32[]{:S(2)}) %collective-permute-start.4) | collective-permute-done | bytes 102432 | tf_op jit(solution)/shard_map/ppermute | solution.py:12
  121.6 4.9 %collective-permute-done.6 = f32[2,2,3,128]{3,2,1,0:T(4,128)S(1)} collective-permute-done((f32[2,2,3,128]{3,2,1,0:T(4,128)S(1)}, f32[2,2,3,128]{3,2,1,0:T(4,128)S(1)}, u32[]{:S(2)}, u32[]{:S(2)}) %collective-permute-start.6) | collective-permute-done | bytes 6176 | tf_op jit(solution)/shard_map/ppermute | solution.py:12
  132.0 39.4 %all-gather.1 = f32[32,6,128]{2,1,0:T(8,128)} all-gather(f32[1,6,128]{2,1,0:T(8,128)S(1)} %reshape.812), channel_id=1, replica_groups=mesh['gx'=4,'gy'=8] {'gx','gy'}, dimensions={0}, use_global_device_ids=true | all-gather | bytes 101376 | tf_op jit(solution)/shard_map/all_gather | solution.py:101
  173.6 3.6 collective-permute-done.8
  184.4 3.2 collective-permute-start.10
  193.0 38.4 %all-reduce.5 = (f32[128]{0:T(128)S(1)}, f32[128]{0:T(128)S(1)}) all-reduce(f32[128]{0:T(128)S(1)} %get-tuple-element.3, f32[128]{0:T(128)S(1)} %get-tuple-element.2), channel_id=1, replica_groups=mesh['gx'=4,'gy'=8] {'gx','gy'}, use_global_device_ids=true, to_apply=%region_1.2 | all-reduce | flops 256 | bytes 2048 | tf_op jit(solution)/shard_map/psum | solution.py:74
  234.4 2.2 collective-permute-start.12
  236.6 4.3 collective-permute-done.12
  244.5 3.0 collective-permute-done.14
  249.3 39.4 %psum.37 = f32[128]{0:T(128)S(1)} all-reduce(f32[128]{0:T(128)} %get-tuple-element.65), channel_id=1, replica_groups=mesh['gx'=4,'gy'=8] {'gx','gy'}, use_global_device_ids=true, to_apply=%region_5.6 | all-reduce | flops 128 | bytes 1024 | tf_op jit(solution)/shard_map/psum | solution.py:74
  292.7 4.5 collective-permute-done.16
  300.4 4.1 collective-permute-done.18
  304.5 3.9 collective-permute-done.19
  308.4 40.7 %all-gather.2 = f32[32,6,128]{2,1,0:T(8,128)} all-gather(f32[1,6,128]{2,1,0:T(8,128)S(1)} %reshape.814), channel_id=1, replica_groups=mesh['gx'=4,'gy'=8] {'gx','gy'}, dimensions={0}, use_global_device_ids=true | all-gather | bytes 101376 | tf_op jit(solution)/shard_map/all_gather | solution.py:101
  352.0 3.6 collective-permute-done.20
  368.1 38.5 %psum.38 = f32[128]{0:T(128)S(1)} all-reduce(f32[128]{0:T(128)S(1)} %get-tuple-element.67), channel_id=1, replica_groups=mesh['gx'=4,'gy'=8] {'gx','gy'}, use_global_device_ids=true, to_apply=%region_7.8 | all-reduce | flops 128 | bytes 1024 | tf_op jit(solution)/shard_map/psum | solution.py:121
  411.8 4.3 collective-permute-done.24
  419.7 3.0 collective-permute-done.26
  423.2 39.6 %psum.39 = f32[128]{0:T(128)S(1)} all-reduce(f32[128]{0:T(128)S(1)} %fusion.16), channel_id=1, replica_groups=mesh['gx'=4,'gy'=8] {'gx','gy'}, use_global_device_ids=true, to_apply=%region_9.10 | all-reduce | flops 128 | bytes 1024 | tf_op jit(solution)/shard_map/psum | solution.py:74
  (223 shorter events, 83.9 us)
Async XLA Ops:
  4.1 96.7 %collective-permute-start.1 = (f32[1,200,128]{2,1,0:T(8,128)S(1)}, f32[1,200,128]{2,1,0:T(8,128)}, u32[]{:S(2)}, u32[]{:S(2)}) collective-permute-start(f32[1,200,128]{2,1,0:T(8,128)S(1)} %get-tuple-element.47), channel_id=1, source_target_pairs={{0,1},{1,2},{2,3},{3,4},{4,5},{5,6},{6,7},{7,0},{8,9},{9,10},{10,1... | collective-permute-start | bytes 307208 | tf_op jit(solution)/shard_map/ppermute | solution.py:12
  4.6 94.4 %collective-permute-start = (f32[1,200,128]{2,1,0:T(8,128)}, f32[1,200,128]{2,1,0:T(8,128)}, u32[]{:S(2)}, u32[]{:S(2)}) collective-permute-start(f32[1,200,128]{2,1,0:T(8,128)} %get-tuple-element.48), channel_id=1, source_target_pairs={{0,8},{8,16},{16,24},{24,0},{1,9},{9,17},{17,25},{25,1},{2,10},{10... | collective-permute-start | bytes 307208 | tf_op jit(solution)/shard_map/ppermute | solution.py:12
  106.5 5.2 %collective-permute-start.2 = (f32[1,200,128]{2,1,0:T(8,128)S(1)}, f32[1,200,128]{2,1,0:T(8,128)S(1)}, u32[]{:S(2)}, u32[]{:S(2)}) collective-permute-start(f32[1,200,128]{2,1,0:T(8,128)S(1)} %get-tuple-element.34), channel_id=1, source_target_pairs={{0,24},{8,0},{16,8},{24,16},{1,25},{9,1},{17,9},{25,17},{2,26},{10... | collective-permute-start | bytes 307208 | tf_op jit(solution)/shard_map/ppermute | solution.py:12
  106.6 5.1 %collective-permute-start.3 = (f32[1,200,128]{2,1,0:T(8,128)S(1)}, f32[1,200,128]{2,1,0:T(8,128)S(1)}, u32[]{:S(2)}, u32[]{:S(2)}) collective-permute-start(f32[1,200,128]{2,1,0:T(8,128)S(1)} %get-tuple-element.35), channel_id=1, source_target_pairs={{0,7},{1,0},{2,1},{3,2},{4,3},{5,4},{6,5},{7,6},{8,15},{9,8},{10,9... | collective-permute-start | bytes 307208 | tf_op jit(solution)/shard_map/ppermute | solution.py:12
  113.1 6.5 %collective-permute-start.4 = (f32[1,200,128]{2,1,0:T(8,128)S(1)}, f32[1,200,128]{2,1,0:T(8,128)S(1)}, u32[]{:S(2)}, u32[]{:S(2)}) collective-permute-start(f32[1,200,128]{2,1,0:T(8,128)S(1)} %get-tuple-element.46), channel_id=1, source_target_pairs={{0,8},{8,16},{16,24},{24,0},{1,9},{9,17},{17,25},{25,1},{2,10},{10... | collective-permute-start | bytes 307208 | tf_op jit(solution)/shard_map/ppermute | solution.py:12
  113.3 6.4 %collective-permute-start.5 = (f32[1,200,128]{2,1,0:T(8,128)S(1)}, f32[1,200,128]{2,1,0:T(8,128)S(1)}, u32[]{:S(2)}, u32[]{:S(2)}) collective-permute-start(f32[1,200,128]{2,1,0:T(8,128)S(1)} %get-tuple-element.45), channel_id=1, source_target_pairs={{0,1},{1,2},{2,3},{3,4},{4,5},{5,6},{6,7},{7,0},{8,9},{9,10},{10,1... | collective-permute-start | bytes 307208 | tf_op jit(solution)/shard_map/ppermute | solution.py:12
  120.9 5.5 %collective-permute-start.6 = (f32[2,2,3,128]{3,2,1,0:T(4,128)S(1)}, f32[2,2,3,128]{3,2,1,0:T(4,128)S(1)}, u32[]{:S(2)}, u32[]{:S(2)}) collective-permute-start(f32[2,2,3,128]{3,2,1,0:T(4,128)S(1)} %fusion.85), channel_id=1, source_target_pairs={{0,8},{8,16},{16,24},{24,0},{1,9},{9,17},{17,25},{25,1},{2,10},{10... | collective-permute-start | bytes 18440 | tf_op jit(solution)/shard_map/ppermute | solution.py:12
  127.0 4.2 collective-permute-start.7
  173.5 3.7 collective-permute-start.8
  184.4 5.8 %collective-permute-start.10 = (f32[1,200,128]{2,1,0:T(8,128)S(1)}, f32[1,200,128]{2,1,0:T(8,128)S(1)}, u32[]{:S(2)}, u32[]{:S(2)}) collective-permute-start(f32[1,200,128]{2,1,0:T(8,128)S(1)} %get-tuple-element.29), channel_id=1, source_target_pairs={{0,24},{8,0},{16,8},{24,16},{1,25},{9,1},{17,9},{25,17},{2,26},{10... | collective-permute-start | bytes 307208 | tf_op jit(solution)/shard_map/ppermute | solution.py:12
  187.5 4.2 collective-permute-start.11
  234.4 6.5 %collective-permute-start.12 = (f32[1,200,128]{2,1,0:T(8,128)S(1)}, f32[1,200,128]{2,1,0:T(8,128)S(1)}, u32[]{:S(2)}, u32[]{:S(2)}) collective-permute-start(f32[1,200,128]{2,1,0:T(8,128)S(1)} %get-tuple-element.44), channel_id=1, source_target_pairs={{0,8},{8,16},{16,24},{24,0},{1,9},{9,17},{17,25},{25,1},{2,10},{10... | collective-permute-start | bytes 307208 | tf_op jit(solution)/shard_map/ppermute | solution.py:12
  236.6 5.0 %collective-permute-start.13 = (f32[1,200,128]{2,1,0:T(8,128)S(1)}, f32[1,200,128]{2,1,0:T(8,128)S(1)}, u32[]{:S(2)}, u32[]{:S(2)}) collective-permute-start(f32[1,200,128]{2,1,0:T(8,128)S(1)} %get-tuple-element.43), channel_id=1, source_target_pairs={{0,1},{1,2},{2,3},{3,4},{4,5},{5,6},{6,7},{7,0},{8,9},{9,10},{10,1... | collective-permute-start | bytes 307208 | tf_op jit(solution)/shard_map/ppermute | solution.py:12
  242.7 4.7 %collective-permute-start.14 = (f32[1,200,128]{2,1,0:T(8,128)S(1)}, f32[1,200,128]{2,1,0:T(8,128)S(1)}, u32[]{:S(2)}, u32[]{:S(2)}) collective-permute-start(f32[1,200,128]{2,1,0:T(8,128)S(1)} %get-tuple-element.24), channel_id=1, source_target_pairs={{0,24},{8,0},{16,8},{24,16},{1,25},{9,1},{17,9},{25,17},{2,26},{10... | collective-permute-start | bytes 307208 | tf_op jit(solution)/shard_map/ppermute | solution.py:12
  290.7 6.5 %collective-permute-start.16 = (f32[1,200,128]{2,1,0:T(8,128)S(1)}, f32[1,200,128]{2,1,0:T(8,128)S(1)}, u32[]{:S(2)}, u32[]{:S(2)}) collective-permute-start(f32[1,200,128]{2,1,0:T(8,128)S(1)} %get-tuple-element.42), channel_id=1, source_target_pairs={{0,8},{8,16},{16,24},{24,0},{1,9},{9,17},{17,25},{25,1},{2,10},{10... | collective-permute-start | bytes 307208 | tf_op jit(solution)/shard_map/ppermute | solution.py:12
  292.7 5.0 %collective-permute-start.17 = (f32[1,200,128]{2,1,0:T(8,128)S(1)}, f32[1,200,128]{2,1,0:T(8,128)S(1)}, u32[]{:S(2)}, u32[]{:S(2)}) collective-permute-start(f32[1,200,128]{2,1,0:T(8,128)S(1)} %get-tuple-element.41), channel_id=1, source_target_pairs={{0,1},{1,2},{2,3},{3,4},{4,5},{5,6},{6,7},{7,0},{8,9},{9,10},{10,1... | collective-permute-start | bytes 307208 | tf_op jit(solution)/shard_map/ppermute | solution.py:12
  299.0 5.5 %collective-permute-start.18 = (f32[2,2,3,128]{3,2,1,0:T(4,128)S(1)}, f32[2,2,3,128]{3,2,1,0:T(4,128)S(1)}, u32[]{:S(2)}, u32[]{:S(2)}) collective-permute-start(f32[2,2,3,128]{3,2,1,0:T(4,128)S(1)} %fusion.83), channel_id=1, source_target_pairs={{0,8},{8,16},{16,24},{24,0},{1,9},{9,17},{17,25},{25,1},{2,10},{10... | collective-permute-start | bytes 18440 | tf_op jit(solution)/shard_map/ppermute | solution.py:12
  304.5 3.9 collective-permute-start.19
  351.9 3.7 collective-permute-start.20
  360.9 5.3 %collective-permute-start.22 = (f32[1,200,128]{2,1,0:T(8,128)S(1)}, f32[1,200,128]{2,1,0:T(8,128)S(1)}, u32[]{:S(2)}, u32[]{:S(2)}) collective-permute-start(f32[1,200,128]{2,1,0:T(8,128)S(1)} %get-tuple-element.19), channel_id=1, source_target_pairs={{0,24},{8,0},{16,8},{24,16},{1,25},{9,1},{17,9},{25,17},{2,26},{10... | collective-permute-start | bytes 307208 | tf_op jit(solution)/shard_map/ppermute | solution.py:12
  362.8 4.1 collective-permute-start.23
  409.6 6.5 %collective-permute-start.24 = (f32[1,200,128]{2,1,0:T(8,128)S(1)}, f32[1,200,128]{2,1,0:T(8,128)S(1)}, u32[]{:S(2)}, u32[]{:S(2)}) collective-permute-start(f32[1,200,128]{2,1,0:T(8,128)S(1)} %get-tuple-element.40), channel_id=1, source_target_pairs={{0,8},{8,16},{16,24},{24,0},{1,9},{9,17},{17,25},{25,1},{2,10},{10... | collective-permute-start | bytes 307208 | tf_op jit(solution)/shard_map/ppermute | solution.py:12
  411.8 5.0 %collective-permute-start.25 = (f32[1,200,128]{2,1,0:T(8,128)S(1)}, f32[1,200,128]{2,1,0:T(8,128)S(1)}, u32[]{:S(2)}, u32[]{:S(2)}) collective-permute-start(f32[1,200,128]{2,1,0:T(8,128)S(1)} %get-tuple-element.39), channel_id=1, source_target_pairs={{0,1},{1,2},{2,3},{3,4},{4,5},{5,6},{6,7},{7,0},{8,9},{9,10},{10,1... | collective-permute-start | bytes 307208 | tf_op jit(solution)/shard_map/ppermute | solution.py:12
  417.9 4.7 %collective-permute-start.26 = (f32[1,200,128]{2,1,0:T(8,128)S(1)}, f32[1,200,128]{2,1,0:T(8,128)S(1)}, u32[]{:S(2)}, u32[]{:S(2)}) collective-permute-start(f32[1,200,128]{2,1,0:T(8,128)S(1)} %get-tuple-element.14), channel_id=1, source_target_pairs={{0,24},{8,0},{16,8},{24,16},{1,25},{9,1},{17,9},{25,17},{2,26},{10... | collective-permute-start | bytes 307208 | tf_op jit(solution)/shard_map/ppermute | solution.py:12
  (30 other events, 829.7 us)
where the time goes:
time: 465 us; the launch traced here: 463 us
  blocking collectives  318 us (68%)
  waiting for transfers between devices  58.1 us (12%)
  matrix products  24.5 us (5%)
  starting transfers between devices  24.4 us (5%)
  other arithmetic  20.7 us (4%)
  local copies, waits for them, and re-layouts  16.7 us (4%)
    psum x3, blocking collectives, energy_total(): return lax.psum(partial_value, ('gx', 'gy'))  117 us
    all_gather x2, blocking collectives, local(): gathered = lax.all_gather(owned, ('gx', 'gy'), axis=0, tiled=True)  80 us
    ppermute x28, waiting for transfers between devices, passed_along(): lax.ppermute(array, axis, [(i, (i + by) % peers) for i in range(peers)])  58.1 us
    all_gather x1, blocking collectives, local(): lax.all_gather(coarse_inverse, ('gx', 'gy'), axis=0, tiled=True)  41.3 us
    unnamed x1, blocking collectives  40.4 us
    psum x1, blocking collectives, local(): curvature = lax.psum(inner_product(direction, product_field), ('gx', 'gy'))  38.5 us
    ppermute x28, starting transfers between devices, passed_along(): lax.ppermute(array, axis, [(i, (i + by) % peers) for i in range(peers)])  24.4 us
  transfers between devices with their start and end apart: 28, of which 20 were waited for; matrix products, arithmetic and copies ran while one was open for 4% of the time, Pallas kernels for 0%

commit v1 on v0

--- a/solution.py
+++ b/solution.py
@@ -33,7 +33,14 @@
     own_ids = jnp.concatenate([local_ids[:, 0], local_ids[-1:, 4]])
     own_dofs = (3 * own_ids[:, None] + jnp.arange(3, dtype=jnp.int32)[None, :]).reshape(-1)
     picked = jnp.take(
-        lax.all_gather(coarse_inverse, ("gx", "gy"), axis=0, tiled=True), own_dofs, axis=1
+        jnp.concatenate(
+            lax.all_to_all(
+                jnp.stack([coarse_inverse] * lax.axis_size(("gx", "gy"))), ("gx", "gy"), 0, 0
+            ),
+            axis=0,
+        ),
+        own_dofs,
+        axis=1,
     )
     every_owner = lax.all_gather(own_ids, ("gx", "gy"), axis=0, tiled=True)
     gathered_dofs = (3 * every_owner[:, None] + jnp.arange(3, dtype=jnp.int32)[None, :]).reshape(-1)

time: 465 us -> 423 us (0.910)
  blocking collectives: 318 us -> 276 us
  starting transfers between devices: 24.4 us -> 31.9 us
    all_gather x1 -> x0, blocking collectives: 41.3 us -> none  [local(): lax.all_gather(coarse_inverse, ('gx', 'gy'), axis=0, tiled=True)]
    all_to_all x0 -> x1, starting transfers between devices: none -> 7.33 us  [local(): lax.all_to_all(jnp.stack([coarse_inverse] * lax.axis_size(('gx', 'gy'))),...]
  transfers between devices with their start and end apart: 28 -> 29, of which waited for: 20 -> 20; matrix products, arithmetic and copies ran while one was open for 4% -> 7% of each run, Pallas kernels for 0% -> 0%
where the time goes in v1:
time: 423 us; the launch traced here: 422 us
  blocking collectives  276 us (65%)
  waiting for transfers between devices  53.8 us (13%)
  starting transfers between devices  31.9 us (8%)
  matrix products  25.1 us (6%)
  other arithmetic  22 us (5%)
  local copies, waits for them, and re-layouts  12.1 us (3%)
    psum x3, blocking collectives, energy_total(): return lax.psum(partial_value, ('gx', 'gy'))  118 us
    all_gather x2, blocking collectives, local(): gathered = lax.all_gather(owned, ('gx', 'gy'), axis=0, tiled=True)  79.4 us
    ppermute x28, waiting for transfers between devices, passed_along(): lax.ppermute(array, axis, [(i, (i + by) % peers) for i in range(peers)])  53.8 us
    unnamed x1, blocking collectives  40.2 us
    psum x1, blocking collectives, local(): curvature = lax.psum(inner_product(direction, product_field), ('gx', 'gy'))  38.4 us
    ppermute x28, starting transfers between devices, passed_along(): lax.ppermute(array, axis, [(i, (i + by) % peers) for i in range(peers)])  24.5 us
    dot_general x5, matrix products, apply_local(): jnp.einsum('snm,smr->snr', matrices, low_field, preferred_element_type=jn...  8.7 us
  transfers between devices with their start and end apart: 29, of which 20 were waited for; matrix products, arithmetic and copies ran while one was open for 7% of the time, Pallas kernels for 0%

profile of v1, /device:TPU:0, one launch (start us, length us, event | category | flops | bytes accessed | tf_op | source)
XLA Modules:
  0.0 422.2 jit_solution(13770739794457885355)
XLA Ops:
  2.2 7.3 %all-to-all-start = ((f32[32,6,192]{2,1,0:T(8,128)}), f32[32,6,192]{2,1,0:T(8,128)S(1)}, u32[]{:S(2)}, u32[]{:S(2)}) async-start(f32[32,6,192]{2,1,0:T(8,128)} %stack.234), calls=%async_computation | async-start | bytes 524288 | tf_op jit(solution)/shard_map/all_to_all | solution.py:37
  19.3 40.2 %all-reduce.4 = s32[64]{0:T(128)S(1)} all-reduce(s32[64]{0:T(128)S(1)} %fusion.96), channel_id=1, replica_groups=mesh['gx'=4,'gy'=8] {'gx','gy'}, use_global_device_ids=true, to_apply=%add.4 | all-reduce | flops 64 | bytes 512
  65.2 2.8 fusion
  68.1 2.4 collective-permute-start.2
  76.8 4.6 %collective-permute-done.4 = f32[1,200,128]{2,1,0:T(8,128)S(1)} collective-permute-done((f32[1,200,128]{2,1,0:T(8,128)S(1)}, f32[1,200,128]{2,1,0:T(8,128)S(1)}, u32[]{:S(2)}, u32[]{:S(2)}) %collective-permute-start.4) | collective-permute-done | bytes 102432 | tf_op jit(solution)/shard_map/ppermute | solution.py:12
  85.5 3.7 collective-permute-done.6
  91.6 2.2 collective-permute-done.7
  93.8 38.4 %all-gather = f32[32,6,128]{2,1,0:T(8,128)S(1)} all-gather(f32[1,6,128]{2,1,0:T(8,128)S(1)} %reshape.816), channel_id=1, replica_groups=mesh['gx'=4,'gy'=8] {'gx','gy'}, dimensions={0}, use_global_device_ids=true | all-gather | bytes 101376 | tf_op jit(solution)/shard_map/all_gather | solution.py:108
  133.2 3.6 collective-permute-done.8
  146.3 2.8 collective-permute-done.10
  150.4 38.8 %all-reduce.5 = (f32[128]{0:T(128)S(1)}, f32[128]{0:T(128)S(1)}) all-reduce(f32[128]{0:T(128)S(1)} %get-tuple-element.3, f32[128]{0:T(128)S(1)} %get-tuple-element.2), channel_id=1, replica_groups=mesh['gx'=4,'gy'=8] {'gx','gy'}, use_global_device_ids=true, to_apply=%region_1.2 | all-reduce | flops 256 | bytes 2048 | tf_op jit(solution)/shard_map/psum | solution.py:81
  194.3 4.3 %collective-permute-done.12 = f32[1,200,128]{2,1,0:T(8,128)S(1)} collective-permute-done((f32[1,200,128]{2,1,0:T(8,128)S(1)}, f32[1,200,128]{2,1,0:T(8,128)S(1)}, u32[]{:S(2)}, u32[]{:S(2)}) %collective-permute-start.12) | collective-permute-done | bytes 102432 | tf_op jit(solution)/shard_map/ppermute | solution.py:12
  202.4 3.0 collective-permute-done.14
  207.2 39.5 %psum.37 = f32[128]{0:T(128)} all-reduce(f32[128]{0:T(128)} %get-tuple-element.65), channel_id=1, replica_groups=mesh['gx'=4,'gy'=8] {'gx','gy'}, use_global_device_ids=true, to_apply=%region_5.6 | all-reduce | flops 128 | bytes 1024 | tf_op jit(solution)/shard_map/psum | solution.py:81
  251.2 4.6 %collective-permute-done.16 = f32[1,200,128]{2,1,0:T(8,128)S(1)} collective-permute-done((f32[1,200,128]{2,1,0:T(8,128)S(1)}, f32[1,200,128]{2,1,0:T(8,128)S(1)}, u32[]{:S(2)}, u32[]{:S(2)}) %collective-permute-start.16) | collective-permute-done | bytes 102432 | tf_op jit(solution)/shard_map/ppermute | solution.py:12
  258.9 4.1 collective-permute-done.18
  263.0 3.9 collective-permute-done.19
  267.0 41.1 %all-gather.1 = f32[32,6,128]{2,1,0:T(8,128)} all-gather(f32[1,6,128]{2,1,0:T(8,128)S(1)} %reshape.818), channel_id=1, replica_groups=mesh['gx'=4,'gy'=8] {'gx','gy'}, dimensions={0}, use_global_device_ids=true | all-gather | bytes 101376 | tf_op jit(solution)/shard_map/all_gather | solution.py:108
  310.9 3.6 collective-permute-done.20
  327.1 38.4 %psum.38 = f32[128]{0:T(128)S(1)} all-reduce(f32[128]{0:T(128)S(1)} %get-tuple-element.67), channel_id=1, replica_groups=mesh['gx'=4,'gy'=8] {'gx','gy'}, use_global_device_ids=true, to_apply=%region_7.8 | all-reduce | flops 128 | bytes 1024 | tf_op jit(solution)/shard_map/psum | solution.py:128
  368.5 2.2 collective-permute-start.24
  370.7 4.3 %collective-permute-done.24 = f32[1,200,128]{2,1,0:T(8,128)S(1)} collective-permute-done((f32[1,200,128]{2,1,0:T(8,128)S(1)}, f32[1,200,128]{2,1,0:T(8,128)S(1)}, u32[]{:S(2)}, u32[]{:S(2)}) %collective-permute-start.24) | collective-permute-done | bytes 102432 | tf_op jit(solution)/shard_map/ppermute | solution.py:12
  378.6 3.0 collective-permute-done.26
  382.1 39.5 %psum.39 = f32[128]{0:T(128)S(1)} all-reduce(f32[128]{0:T(128)S(1)} %fusion.16), channel_id=1, replica_groups=mesh['gx'=4,'gy'=8] {'gx','gy'}, use_global_device_ids=true, to_apply=%region_9.10 | all-reduce | flops 128 | bytes 1024 | tf_op jit(solution)/shard_map/psum | solution.py:81
  (219 shorter events, 82.4 us)
Async XLA Ops:
  2.2 82.4 %all-to-all-start = ((f32[32,6,192]{2,1,0:T(8,128)}), f32[32,6,192]{2,1,0:T(8,128)S(1)}, u32[]{:S(2)}, u32[]{:S(2)}) async-start(f32[32,6,192]{2,1,0:T(8,128)} %stack.234), calls=%async_computation | async-start | bytes 524288 | tf_op jit(solution)/shard_map/all_to_all | solution.py:37
  12.8 51.4 %collective-permute-start.1 = (f32[1,200,128]{2,1,0:T(8,128)S(1)}, f32[1,200,128]{2,1,0:T(8,128)}, u32[]{:S(2)}, u32[]{:S(2)}) collective-permute-start(f32[1,200,128]{2,1,0:T(8,128)S(1)} %get-tuple-element.47), channel_id=1, source_target_pairs={{0,1},{1,2},{2,3},{3,4},{4,5},{5,6},{6,7},{7,0},{8,9},{9,10},{10,1... | collective-permute-start | bytes 307208 | tf_op jit(solution)/shard_map/ppermute | solution.py:12
  13.0 50.2 %collective-permute-start = (f32[1,200,128]{2,1,0:T(8,128)}, f32[1,200,128]{2,1,0:T(8,128)}, u32[]{:S(2)}, u32[]{:S(2)}) collective-permute-start(f32[1,200,128]{2,1,0:T(8,128)} %get-tuple-element.48), channel_id=1, source_target_pairs={{0,8},{8,16},{16,24},{24,0},{1,9},{9,17},{17,25},{25,1},{2,10},{10... | collective-permute-start | bytes 307208 | tf_op jit(solution)/shard_map/ppermute | solution.py:12
  68.1 4.7 %collective-permute-start.2 = (f32[1,200,128]{2,1,0:T(8,128)S(1)}, f32[1,200,128]{2,1,0:T(8,128)S(1)}, u32[]{:S(2)}, u32[]{:S(2)}) collective-permute-start(f32[1,200,128]{2,1,0:T(8,128)S(1)} %get-tuple-element.34), channel_id=1, source_target_pairs={{0,24},{8,0},{16,8},{24,16},{1,25},{9,1},{17,9},{25,17},{2,26},{10... | collective-permute-start | bytes 307208 | tf_op jit(solution)/shard_map/ppermute | solution.py:12
  74.8 6.7 %collective-permute-start.4 = (f32[1,200,128]{2,1,0:T(8,128)S(1)}, f32[1,200,128]{2,1,0:T(8,128)S(1)}, u32[]{:S(2)}, u32[]{:S(2)}) collective-permute-start(f32[1,200,128]{2,1,0:T(8,128)S(1)} %get-tuple-element.46), channel_id=1, source_target_pairs={{0,8},{8,16},{16,24},{24,0},{1,9},{9,17},{17,25},{25,1},{2,10},{10... | collective-permute-start | bytes 307208 | tf_op jit(solution)/shard_map/ppermute | solution.py:12
  74.9 6.6 %collective-permute-start.5 = (f32[1,200,128]{2,1,0:T(8,128)S(1)}, f32[1,200,128]{2,1,0:T(8,128)S(1)}, u32[]{:S(2)}, u32[]{:S(2)}) collective-permute-start(f32[1,200,128]{2,1,0:T(8,128)S(1)} %get-tuple-element.45), channel_id=1, source_target_pairs={{0,1},{1,2},{2,3},{3,4},{4,5},{5,6},{6,7},{7,0},{8,9},{9,10},{10,1... | collective-permute-start | bytes 307208 | tf_op jit(solution)/shard_map/ppermute | solution.py:12
  83.4 5.8 %collective-permute-start.6 = (f32[2,2,3,128]{3,2,1,0:T(4,128)}, f32[2,2,3,128]{3,2,1,0:T(4,128)}, u32[]{:S(2)}, u32[]{:S(2)}) collective-permute-start(f32[2,2,3,128]{3,2,1,0:T(4,128)} %fusion.85), channel_id=1, source_target_pairs={{0,8},{8,16},{16,24},{24,0},{1,9},{9,17},{17,25},{25,1},{2,10},{10... | collective-permute-start | bytes 18440 | tf_op jit(solution)/shard_map/ppermute | solution.py:12
  89.9 3.9 collective-permute-start.7
  133.1 3.7 collective-permute-start.8
  143.8 5.3 %collective-permute-start.10 = (f32[1,200,128]{2,1,0:T(8,128)S(1)}, f32[1,200,128]{2,1,0:T(8,128)S(1)}, u32[]{:S(2)}, u32[]{:S(2)}) collective-permute-start(f32[1,200,128]{2,1,0:T(8,128)S(1)} %get-tuple-element.29), channel_id=1, source_target_pairs={{0,24},{8,0},{16,8},{24,16},{1,25},{9,1},{17,9},{25,17},{2,26},{10... | collective-permute-start | bytes 307208 | tf_op jit(solution)/shard_map/ppermute | solution.py:12
  145.7 3.5 collective-permute-start.11
  192.1 6.5 %collective-permute-start.12 = (f32[1,200,128]{2,1,0:T(8,128)S(1)}, f32[1,200,128]{2,1,0:T(8,128)S(1)}, u32[]{:S(2)}, u32[]{:S(2)}) collective-permute-start(f32[1,200,128]{2,1,0:T(8,128)S(1)} %get-tuple-element.44), channel_id=1, source_target_pairs={{0,8},{8,16},{16,24},{24,0},{1,9},{9,17},{17,25},{25,1},{2,10},{10... | collective-permute-start | bytes 307208 | tf_op jit(solution)/shard_map/ppermute | solution.py:12
  194.3 5.0 %collective-permute-start.13 = (f32[1,200,128]{2,1,0:T(8,128)S(1)}, f32[1,200,128]{2,1,0:T(8,128)S(1)}, u32[]{:S(2)}, u32[]{:S(2)}) collective-permute-start(f32[1,200,128]{2,1,0:T(8,128)S(1)} %get-tuple-element.43), channel_id=1, source_target_pairs={{0,1},{1,2},{2,3},{3,4},{4,5},{5,6},{6,7},{7,0},{8,9},{9,10},{10,1... | collective-permute-start | bytes 307208 | tf_op jit(solution)/shard_map/ppermute | solution.py:12
  200.5 4.9 %collective-permute-start.14 = (f32[1,200,128]{2,1,0:T(8,128)S(1)}, f32[1,200,128]{2,1,0:T(8,128)S(1)}, u32[]{:S(2)}, u32[]{:S(2)}) collective-permute-start(f32[1,200,128]{2,1,0:T(8,128)S(1)} %get-tuple-element.24), channel_id=1, source_target_pairs={{0,24},{8,0},{16,8},{24,16},{1,25},{9,1},{17,9},{25,17},{2,26},{10... | collective-permute-start | bytes 307208 | tf_op jit(solution)/shard_map/ppermute | solution.py:12
  249.3 6.5 %collective-permute-start.16 = (f32[1,200,128]{2,1,0:T(8,128)S(1)}, f32[1,200,128]{2,1,0:T(8,128)S(1)}, u32[]{:S(2)}, u32[]{:S(2)}) collective-permute-start(f32[1,200,128]{2,1,0:T(8,128)S(1)} %get-tuple-element.42), channel_id=1, source_target_pairs={{0,8},{8,16},{16,24},{24,0},{1,9},{9,17},{17,25},{25,1},{2,10},{10... | collective-permute-start | bytes 307208 | tf_op jit(solution)/shard_map/ppermute | solution.py:12
  251.2 5.0 %collective-permute-start.17 = (f32[1,200,128]{2,1,0:T(8,128)S(1)}, f32[1,200,128]{2,1,0:T(8,128)S(1)}, u32[]{:S(2)}, u32[]{:S(2)}) collective-permute-start(f32[1,200,128]{2,1,0:T(8,128)S(1)} %get-tuple-element.41), channel_id=1, source_target_pairs={{0,1},{1,2},{2,3},{3,4},{4,5},{5,6},{6,7},{7,0},{8,9},{9,10},{10,1... | collective-permute-start | bytes 307208 | tf_op jit(solution)/shard_map/ppermute | solution.py:12
  257.5 5.5 %collective-permute-start.18 = (f32[2,2,3,128]{3,2,1,0:T(4,128)S(1)}, f32[2,2,3,128]{3,2,1,0:T(4,128)S(1)}, u32[]{:S(2)}, u32[]{:S(2)}) collective-permute-start(f32[2,2,3,128]{3,2,1,0:T(4,128)S(1)} %fusion.83), channel_id=1, source_target_pairs={{0,8},{8,16},{16,24},{24,0},{1,9},{9,17},{17,25},{25,1},{2,10},{10... | collective-permute-start | bytes 18440 | tf_op jit(solution)/shard_map/ppermute | solution.py:12
  263.0 3.9 collective-permute-start.19
  310.8 3.7 collective-permute-start.20
  319.9 5.3 %collective-permute-start.22 = (f32[1,200,128]{2,1,0:T(8,128)S(1)}, f32[1,200,128]{2,1,0:T(8,128)S(1)}, u32[]{:S(2)}, u32[]{:S(2)}) collective-permute-start(f32[1,200,128]{2,1,0:T(8,128)S(1)} %get-tuple-element.19), channel_id=1, source_target_pairs={{0,24},{8,0},{16,8},{24,16},{1,25},{9,1},{17,9},{25,17},{2,26},{10... | collective-permute-start | bytes 307208 | tf_op jit(solution)/shard_map/ppermute | solution.py:12
  321.7 4.1 collective-permute-start.23
  368.5 6.5 %collective-permute-start.24 = (f32[1,200,128]{2,1,0:T(8,128)S(1)}, f32[1,200,128]{2,1,0:T(8,128)S(1)}, u32[]{:S(2)}, u32[]{:S(2)}) collective-permute-start(f32[1,200,128]{2,1,0:T(8,128)S(1)} %get-tuple-element.40), channel_id=1, source_target_pairs={{0,8},{8,16},{16,24},{24,0},{1,9},{9,17},{17,25},{25,1},{2,10},{10... | collective-permute-start | bytes 307208 | tf_op jit(solution)/shard_map/ppermute | solution.py:12
  370.7 5.0 %collective-permute-start.25 = (f32[1,200,128]{2,1,0:T(8,128)S(1)}, f32[1,200,128]{2,1,0:T(8,128)S(1)}, u32[]{:S(2)}, u32[]{:S(2)}) collective-permute-start(f32[1,200,128]{2,1,0:T(8,128)S(1)} %get-tuple-element.39), channel_id=1, source_target_pairs={{0,1},{1,2},{2,3},{3,4},{4,5},{5,6},{6,7},{7,0},{8,9},{9,10},{10,1... | collective-permute-start | bytes 307208 | tf_op jit(solution)/shard_map/ppermute | solution.py:12
  376.9 4.7 %collective-permute-start.26 = (f32[1,200,128]{2,1,0:T(8,128)S(1)}, f32[1,200,128]{2,1,0:T(8,128)S(1)}, u32[]{:S(2)}, u32[]{:S(2)}) collective-permute-start(f32[1,200,128]{2,1,0:T(8,128)S(1)} %get-tuple-element.14), channel_id=1, source_target_pairs={{0,24},{8,0},{16,8},{24,16},{1,25},{9,1},{17,9},{25,17},{2,26},{10... | collective-permute-start | bytes 307208 | tf_op jit(solution)/shard_map/ppermute | solution.py:12
  (28 other events, 780.5 us)
